TPU v7x, 256 devices: a whole 4x4x8 slice. The times are simulated.
256 devices in a mesh: replica: 32 (over y, z), shard: 8 (over x, core).
Axes of the slice: x: 4, y: 4, z: 8, core: 2. Of those that a mesh axis runs over, the one named last changes fastest.
Arguments:
- outer_params: float32 [1024, 4096], P('shard'), may hold values from -6 to 6, as said below
- local_params: bfloat16 [32, 1024, 4096], P('replica', 'shard'), may hold values from -70 to 70
- momentum: float32 [1024, 4096], P('shard'), may hold values from -6 to 6
Outputs:
- params_next: float32 [1024, 4096], P('shard')
- momentum_next: float32 [1024, 4096], P('shard')
- block_scales: float32 [32, 1024], P(None, 'shard')
Inputs may be any that keep to these rules, and one draw needn't show every extreme that they name: `outer_params`: outer parameters of order one.
All inputs are finite; a program needn't handle non-finite values.
Results may differ from a plain program's by a relative error of at most 0.005.
Values may be sent and summed in bfloat16 or wider, within the bound.
A program may use at most 64 MiB of HBM per device.

v0:
```python
import math

import jax
import jax.numpy as jnp
from jax import lax
from jax.sharding import Mesh
from jax.sharding import PartitionSpec as P

BLOCK = 128
REPLICA = ("replica_0", "replica_1")
REPLICA_SHARD = ("replica_0", "replica_1", "shard_0", "shard_1")
SHARD = ("shard_0", "shard_1")


epsilon = 1e-06
clip_level = 0.5
outer_rate = 0.7
outer_decay = 0.9
grid_levels = 7.0


def copy_for_each(x, axis):
    copies = jnp.broadcast_to(x, (lax.axis_size(axis), *x.shape))
    return lax.all_to_all(copies, axis, split_axis=0, concat_axis=0, tiled=True)


def taken_together(x, axis):
    everything = copy_for_each(x, axis)
    return jnp.max(everything, axis=0)


def in_blocks(x, dim, devices):
    dims = x.shape
    pieces = x.reshape(*dims[:dim], devices, dims[dim] // devices, *dims[dim + 1 :])
    return jnp.moveaxis(pieces, dim, 0)


def summed_on_arrival(x, axis, dim):
    pieces = in_blocks(x, dim, lax.axis_size(axis))
    arrived = lax.all_to_all(pieces, axis, split_axis=0, concat_axis=0, tiled=True)
    return arrived.astype(jnp.float32).sum(axis=0)


def over_axes(x, axes):
    for axis in axes:
        x = lax.psum(x, axis)
    return x


def smooth_step(values):
    return values - jnp.sin(2.0 * math.pi * values) / (2.0 * math.pi)


def smooth_round(values):
    return smooth_step(smooth_step(values))


def block_max(values):
    return jnp.max(
        jnp.abs(values).reshape(values.shape[0], values.shape[1] // BLOCK, BLOCK), axis=2
    )


def per_device(outer_params, local_params, momentum):
    workers = lax.axis_size(REPLICA)
    row_count = outer_params.shape[0]
    col_count = outer_params.shape[1]
    deltas = outer_params - local_params[0].astype(jnp.float32)
    absmax = taken_together(block_max(deltas), REPLICA)
    spread_scale = jnp.repeat(absmax + epsilon, BLOCK, axis=1)
    encoded = smooth_round(grid_levels * deltas / spread_scale).astype(jnp.bfloat16)
    summed_rows = summed_on_arrival(
        (spread_scale * encoded.astype(jnp.float32) / grid_levels).astype(jnp.bfloat16), REPLICA, 0
    )
    gradient_slice = summed_rows / workers
    square_total = over_axes(jnp.sum(gradient_slice * gradient_slice), REPLICA_SHARD)
    entry_count = row_count * lax.axis_size(SHARD) * col_count
    root_mean = jnp.sqrt(square_total / entry_count + epsilon)
    factor = jnp.minimum(1.0, clip_level / root_mean)
    gradient = lax.all_gather(gradient_slice, REPLICA, axis=0, tiled=True)
    clipped = factor * gradient
    momentum_next = outer_decay * momentum + clipped
    params_next = outer_params - outer_rate * (clipped + outer_decay * momentum_next)
    return (params_next, momentum_next, absmax.T)


def solution(mesh):
    finer = Mesh(mesh.devices.reshape(4, 8, 4, 2), ("replica_0", "replica_1", "shard_0", "shard_1"))
    placed = (P(SHARD, None), P(REPLICA, SHARD, None), P(SHARD, None))
    return jax.shard_map(
        per_device,
        mesh=finer,
        in_specs=placed,
        out_specs=(P(SHARD, None), P(SHARD, None), P(None, SHARD)),
        check_vma=False,
    )
```

profile of v0, /device:TPU:2, one launch (start us, length us, event | category | flops | bytes accessed | tf_op | source)
XLA Modules:
  0.0 185.8 jit_solution(7357414329227839950)
XLA Ops:
  7.2 0.0 all-gather.3.cloned.1.call-start
  7.2 2.1 %abs_bitcast_fusion = f32[16,8,32,128]{3,1,2,0:T(8,128)S(1)} fusion(f32[128,4096]{1,0:T(8,128)} %param.3, bf16[1,128,4096]{2,1,0:T(8,128)(2,1)} %param.4), kind=kLoop, calls=%fused_computation.9 | loop fusion | flops 1572864 | bytes 5242880
  9.3 0.4 copy.10
  9.7 0.6 reduce_max.18
  10.3 0.1 copy.8
  10.4 0.1 broadcast_in_dim.6
  10.5 28.4 %all_to_all.10 = f32[32,128,32]{1,2,0:T(8,128)} all-to-all(f32[32,128,32]{1,2,0:T(8,128)S(1)} %broadcast_in_dim.6), channel_id=1, replica_groups=mesh['replica_0'=4,'replica_1'=8,'shard_0'=4,'shard_1'=2] {'replica_0','..., dimensions={0} | all-to-all | bytes 1048576 | tf_op jit(solution)/shard_map/all_to_all | solution.py:24
  38.8 1.1 reduce_max.19
  39.9 0.1 copy.9
  40.0 0.6 broadcast_in_dim.7
  40.6 15.7 %fusion.1 = bf16[128,4096]{1,0:T(8,128)(2,1)} fusion(f32[16,8,32,128]{3,2,1,0:T(8,128)S(1)} %bitcast.24, f32[128,4096]{1,0:T(8,128)S(1)} %copy-done, bf16[1,128,4096]{2,1,0:T(8,128)(2,1)S(1)} %copy-done.1), kind=kLoop, calls=%fused_computation.3 | loop fusion | flops 7864320 | bytes 6291456 | tf_op jit(solution)/shard_map/convert_element_type | solution.py:73
  56.4 1.5 reshape.19
  57.9 33.7 %all_to_all.11 = bf16[32,4,4096]{2,1,0:T(4,128)(2,1)S(1)} all-to-all(bf16[32,4,4096]{2,1,0:T(4,128)(2,1)S(1)} %reshape.19), channel_id=1, replica_groups=mesh['replica_0'=4,'replica_1'=8,'shard_0'=4,'shard_1'=2] {'replica_0','..., dimensions={0} | all-to-all | bytes 2097152 | tf_op jit(solution)/shard_map/all_to_all | solution.py:40
  91.5 0.4 convert_reduce_fusion
  92.0 1.2 multiply_reduce_fusion
  93.2 0.0 all-gather.3.cloned.1.call-update
  93.2 9.2 %psum.28 = f32[]{:T(128)} all-reduce(f32[]{:T(128)} %get-tuple-element.5), channel_id=1, replica_groups=mesh['replica_0'=4,'replica_1'=8,'shard_0'=4,'shard_1'=2] {'replica_0'}, use_global_device_ids=true, to_apply=%region_4.0 | all-reduce | flops 1 | bytes 8 | tf_op jit(solution)/shard_map/psum | solution.py:46
  102.4 16.8 %psum.29 = f32[]{:T(128)} all-reduce(f32[]{:T(128)} %psum.28), channel_id=1, replica_groups=mesh['replica_0'=4,'replica_1'=8,'shard_0'=4,'shard_1'=2] {'replica_1'}, use_global_device_ids=true, to_apply=%region_5.0 | all-reduce | flops 1 | bytes 8 | tf_op jit(solution)/shard_map/psum | solution.py:46
  119.2 9.2 %psum.30 = f32[]{:T(128)} all-reduce(f32[]{:T(128)} %psum.29), channel_id=1, replica_groups=mesh['replica_0'=4,'replica_1'=8,'shard_0'=4,'shard_1'=2] {'shard_0'}, use_global_device_ids=true, to_apply=%region_6.0 | all-reduce | flops 1 | bytes 8 | tf_op jit(solution)/shard_map/psum | solution.py:46
  128.4 3.1 %psum.31 = f32[]{:T(128)} all-reduce(f32[]{:T(128)} %psum.30), channel_id=1, replica_groups=mesh['replica_0'=4,'replica_1'=8,'shard_0'=4,'shard_1'=2] {'shard_1'}, use_global_device_ids=true, to_apply=%region_7.0 | all-reduce | flops 1 | bytes 8 | tf_op jit(solution)/shard_map/psum | solution.py:46
  132.2 35.7 %all-gather.3.cloned.1.call-done = f32[32,4,4096]{2,1,0:T(4,128)} async-done(((f32[1,4,4096]{2,1,0:T(4,128)}), f32[32,4,4096]{2,1,0:T(4,128)}) %all-gather.3.cloned.1.call-update) | async-done | bytes 2097168 | tf_op jit(solution)/shard_map/all_gather | solution.py:80
  167.9 3.1 %broadcast_multiply_fusion = f32[16,8,4096]{2,1,0:T(8,128)} fusion(f32[16,8,4096]{2,1,0:T(8,128)} %bitcast.27, f32[]{:T(128)S(6)} %min_shard_map.3), kind=kLoop, calls=%fused_computation.10 | loop fusion | flops 524288 | bytes 4194308 | tf_op jit(solution)/shard_map/mul | solution.py:81
  171.0 2.9 %reshape.24 = f32[128,4096]{1,0:T(8,128)} reshape(f32[32,4,4096]{2,1,0:T(4,128)} %bitcast.25) | data formatting | bytes 4194304 | tf_op jit(solution)/shard_map/mul | solution.py:81
  173.9 5.0 %multiply_subtract_fusion = (f32[128,4096]{1,0:T(8,128)}, f32[128,4096]{1,0:T(8,128)}) fusion(f32[128,4096]{1,0:T(8,128)S(1)} %copy-done, f32[128,4096]{1,0:T(8,128)} %reshape.24, f32[128,4096]{1,0:T(8,128)} %param.5), kind=kLoop, calls=%fused_computation.5 | loop fusion | flops 3145728 | bytes 10485760 | tf_op jit(solution)/shard_map/sub | solution.py:83
  (7 shorter events, 0.0 us)
Async XLA Ops:
  7.2 160.7 %all-gather.3.cloned.1.call-start = ((), (), s32[]{:S(2)}) async-start(), calls=%async_computation.2 | async-start | bytes 2162688 | tf_op jit(solution)/shard_map/all_gather | solution.py:80
  10.4 30.3 %copy-start = (f32[128,4096]{1,0:T(8,128)S(1)}, f32[128,4096]{1,0:T(8,128)}, u32[]{:S(2)}) copy-start(f32[128,4096]{1,0:T(8,128)} %param.3) | copy-start | bytes 6291460
  10.4 30.3 %copy-start.1 = (bf16[1,128,4096]{2,1,0:T(8,128)(2,1)S(1)}, bf16[1,128,4096]{2,1,0:T(8,128)(2,1)}, u32[]{:S(2)}) copy-start(bf16[1,128,4096]{2,1,0:T(8,128)(2,1)} %param.4) | copy-start | bytes 3145732
  39.9 16.5 %copy-start.2 = (f32[128,32]{0,1:T(8,128)}, f32[128,32]{0,1:T(8,128)S(1)}, u32[]{:S(2)}) copy-start(f32[128,32]{0,1:T(8,128)S(1)} %reduce_max.19) | copy-start | bytes 49156
Sparse Core Ops, SparseCore 0:
  93.4 74.4 all-gather.2
where the time goes:
time: 186 us
  blocking collectives  100 us (54%)
  waiting for transfers between devices  35.7 us (19%)
  other arithmetic  29.4 us (16%)
  between operations  14.8 us (8%)
  local copies, waits for them, and re-layouts  5.59 us (3%)
    psum x4, blocking collectives, over_axes(): x = lax.psum(x, axis)  38.2 us
    all_gather x1, waiting for transfers between devices, per_device(): gradient = lax.all_gather(gradient_slice, REPLICA, axis=0, tiled=True)  35.7 us
    all_to_all x1, blocking collectives, summed_on_arrival(): lax.all_to_all(pieces, axis, split_axis=0, concat_axis=0, tiled=True)  33.7 us
    all_to_all x1, blocking collectives, copy_for_each(): return lax.all_to_all(copies, axis, split_axis=0, concat_axis=0, tiled=True)  28.4 us
    convert_element_type x1, other arithmetic, per_device(): (spread_scale * encoded.astype(jnp.float32) / grid_levels).astype(jnp.bfl...  15.7 us
    sub x1, other arithmetic, per_device(): outer_params - outer_rate * (clipped + outer_decay * momentum_next)  5.05 us
  transfers between devices with their start and end apart: 1, of which 1 were waited for; matrix products, arithmetic and copies ran while one was open for 0% of the time, Pallas kernels for 0%

commit v1 on v0

v1 whole, which is shorter than its diff:
```python
import jax
import jax.numpy as jnp
from jax import lax
from jax.experimental import pallas as pl
from jax.experimental.pallas import tpu as pltpu
from jax.sharding import Mesh
from jax.sharding import PartitionSpec as P

F32, BF16 = jnp.float32, jnp.bfloat16
MESH = pl.DeviceIdType.MESH
BLOCK = 128
AXES = ("y", "z", "x", "core")
SIZES = {"y": 4, "z": 8, "x": 4, "core": 2}
REPLICA = ("y", "z")
SHARD = ("x", "core")
NY, NZ = SIZES["y"], SIZES["z"]
WORKERS = NY * NZ

epsilon = 1e-06
clip_level = 0.5
outer_rate = 0.7
outer_decay = 0.9
grid_levels = 7.0

CURVE = (
    6.579736058540756,
    -12.987862704441794,
    12.207700561043827,
    -6.688877467338575,
    2.372163287039885,
    -0.5163244078344457,
)

Y_STEPS = (2, 1, 3)
Z_FAR = (4, 3, 5, 2, 6, 1, 7)
Z_NEAR = (1, 7, 2, 6, 3, 5, 4)
CELL = tuple((a, b) for a in range(4) for b in range(2) if (a, b) != (0, 0))


def curve(r):
    t = r * r
    p = CURVE[-1]
    for c in CURVE[-2::-1]:
        p = p * t + c
    return (r * t) * p


def smooth_round(v):
    whole = jnp.round(v)
    return whole + curve(curve(v - whole))


def kernel(
    outer_hbm, local_hbm, momentum_hbm, params_ref, momentum_ref, scales_ref,
    outer_v, local_v, momentum_v, maxima, maxima_y, max_own, maxima_z, max_row, max_all,
    inverse, spread, raw_y, partial, total, parts_z, gathered, squares, squares_in,
    load_sem, my_s, my_r, mz_s, mz_r, ma_s, ma_r, raw_s, raw_r, part_s, part_r,
    gz_s, gz_r, gy_s, gy_r, sq_s, sq_r,
):
    y, z = lax.axis_index("y"), lax.axis_index("z")
    x, core = lax.axis_index("x"), lax.axis_index("core")
    at = {"y": y, "z": z, "x": x, "core": core}
    rows, cols = outer_v.shape
    nr, nc = rows // NY, cols // NZ
    per = nc // BLOCK
    entry_count = rows * cols * SIZES["x"] * SIZES["core"]

    def peer(**steps):
        return {k: lax.rem(at[k] + s, SIZES[k]) for k, s in steps.items()}

    def send(src, dst, ss, rs, **steps):
        return pltpu.make_async_remote_copy(
            src_ref=src, dst_ref=dst, send_sem=ss, recv_sem=rs,
            device_id=peer(**steps), device_id_type=MESH,
        )

    def row_of(g):
        return pl.ds(pl.multiple_of(g * nr, nr), nr)

    def col_of(g):
        return pl.ds(pl.multiple_of(g * nc, nc), nc)

    barrier = pltpu.get_barrier_semaphore()
    friends = (
        [dict(y=s) for s in range(1, NY)]
        + [dict(z=s) for s in range(1, NZ)]
        + [dict(x=a, core=b) for a, b in CELL]
    )
    for f in friends:
        pl.semaphore_signal(barrier, inc=1, device_id=peer(**f), device_id_type=MESH)

    loads = []
    for g in range(NY):
        loads.append([
            pltpu.make_async_copy(
                local_hbm.at[0, pl.ds(g * nr, nr)], local_v.at[pl.ds(g * nr, nr)], load_sem.at[g]
            ),
            pltpu.make_async_copy(
                outer_hbm.at[pl.ds(g * nr, nr)], outer_v.at[pl.ds(g * nr, nr)], load_sem.at[NY + g]
            ),
        ])
    for pair in loads:
        for c in pair:
            c.start()
    load_momentum = pltpu.make_async_copy(momentum_hbm, momentum_v, load_sem.at[2 * NY])
    load_momentum.start()

    for g in range(NY):
        for c in loads[g]:
            c.wait()

        def block_max(p, _, g=g):
            blocks = []
            for j in range(per):
                where = (pl.ds(g * nr, nr), pl.ds(pl.multiple_of(p * nc + j * BLOCK, BLOCK), BLOCK))
                blocks.append(jnp.abs(outer_v[where] - local_v[where].astype(F32)))
            stack = jnp.concatenate(blocks, axis=0)
            maxima[g, pl.ds(p, 1), :] = jnp.max(stack.T, axis=0, keepdims=True)
            return 0

        lax.fori_loop(0, NZ, block_max, 0)

    pl.semaphore_wait(barrier, len(friends))

    my = [
        send(maxima.at[lax.rem(y + s, NY)], maxima_y.at[i], my_s.at[i], my_r.at[i], y=s)
        for i, s in enumerate(Y_STEPS)
    ]
    for c in my:
        c.start()

    order = (4, 3, 5, 2, 6, 1, 7, 0)

    def piece_of(i):
        return lax.rem(z + order[i], NZ)

    raw = {}
    for i in range(NZ):
        for k, s in enumerate(Y_STEPS):
            raw[i, k] = send(
                local_v.at[row_of(lax.rem(y + s, NY)), col_of(piece_of(i))],
                raw_y.at[k, i], raw_s.at[k, i], raw_r.at[k, i], y=s,
            )
            raw[i, k].start()

    for c in my:
        c.wait_recv()
    m = maxima[y]
    for i in range(len(Y_STEPS)):
        m = jnp.maximum(m, maxima_y[i])
    max_own[...] = m
    mz = [
        send(max_own, maxima_z.at[i], mz_s.at[i], mz_r.at[i], z=s) for i, s in enumerate(Z_FAR)
    ]
    for c in mz:
        c.start()
    for c in mz:
        c.wait_recv()
    m = max_own[...]
    for i in range(len(Z_FAR)):
        m = jnp.maximum(m, maxima_z[i])
    max_row[...] = m
    ma = [
        send(max_row, max_all.at[y], ma_s.at[i], ma_r.at[i], y=s) for i, s in enumerate(Y_STEPS)
    ]
    for c in ma:
        c.start()
    max_all[y] = m

    inverse_rows = grid_levels / (m + epsilon)
    for p in range(NZ):
        inverse[p] = jnp.broadcast_to(inverse_rows[p : p + 1, :], (BLOCK, BLOCK)).T
    max_own_piece = max_row[pl.ds(z, 1), :] + epsilon
    spread[...] = jnp.broadcast_to(max_own_piece, (BLOCK, BLOCK)).T

    part = {}
    for i in range(NZ):
        p = piece_of(i)
        for k in range(len(Y_STEPS)):
            raw[i, k].wait_recv()

        def encode(j, _, i=i, p=p):
            lanes = pl.ds(pl.multiple_of(j * BLOCK, BLOCK), BLOCK)
            columns = pl.ds(pl.multiple_of(p * nc + j * BLOCK, BLOCK), BLOCK)
            o = outer_v[row_of(y), columns]
            inv = inverse[p, pl.ds(pl.multiple_of(j * nr, nr), nr), :]
            acc = jnp.zeros((nr, BLOCK), F32)
            for w in range(NY):
                local = local_v[row_of(y), columns] if w == 0 else raw_y[w - 1, i, :, lanes]
                v = (o - local.astype(F32)) * inv
                acc += smooth_round(v).astype(BF16).astype(F32)
            if i < NZ - 1:
                partial[i, :, lanes] = acc.astype(BF16)
            else:
                total[:, lanes] = acc
            return 0

        lax.fori_loop(0, per, encode, 0)
        if i < NZ - 1:
            part[i] = send(
                partial.at[i], parts_z.at[i], part_s.at[i], part_r.at[i], z=order[i]
            )
            part[i].start()

    for i in range(NZ - 1):
        part[i].wait_recv()

    sq = jnp.zeros((8, BLOCK), F32)
    for j in range(per):
        lanes = pl.ds(j * BLOCK, BLOCK)
        acc = total[:, lanes]
        for i in range(NZ - 1):
            acc += parts_z[i, :, lanes].astype(F32)
        g = acc * (spread[pl.ds(j * nr, nr), :] * (1.0 / (grid_levels * WORKERS)))
        gathered[y, z, :, lanes] = g.astype(BF16)
        g2 = g * g
        for r in range(nr // 8):
            sq += g2[r * 8 : r * 8 + 8]
    squares[0] = sq

    gz = [
        send(gathered.at[y, z], gathered.at[y, z], gz_s.at[i], gz_r.at[i], z=s)
        for i, s in enumerate(Z_NEAR)
    ]
    qz = [
        send(squares.at[0], squares_in.at[i], sq_s.at[i], sq_r.at[i], z=s)
        for i, s in enumerate(Z_NEAR)
    ]
    gy = {}

    def spread_y(i, source):
        for k, s in enumerate(Y_STEPS):
            ref = gathered.at[y, source]
            gy[i, k] = send(ref, ref, gy_s.at[k, i], gy_r.at[k, i], y=s)
            gy[i, k].start()

    for c, q in zip(gz, qz):
        q.start()
        c.start()
    spread_y(0, z)
    for i, s in enumerate(Z_NEAR):
        source = lax.rem(z + NZ - s, NZ)
        ref = gathered.at[y, source]
        send(ref, ref, gz_s.at[i], gz_r.at[i], z=s).wait_recv()
        spread_y(i + 1, source)

    def add_up(slot, first, copies):
        for c in copies:
            c.wait_recv()
        acc = squares[slot]
        for i in range(len(copies)):
            acc += squares_in[first + i]
        squares[slot + 1] = acc

    add_up(0, 0, qz)
    qy = [
        send(squares.at[1], squares_in.at[7 + i], sq_s.at[7 + i], sq_r.at[7 + i], y=s)
        for i, s in enumerate(Y_STEPS)
    ]
    for q in qy:
        q.start()
    add_up(1, 7, qy)
    qc = [
        send(squares.at[2], squares_in.at[10 + i], sq_s.at[10 + i], sq_r.at[10 + i], x=a, core=b)
        for i, (a, b) in enumerate(CELL)
    ]
    for q in qc:
        q.start()
    add_up(2, 10, qc)
    square_total = jnp.sum(squares[3], axis=(0, 1), keepdims=True)
    root_mean = jnp.sqrt(square_total / entry_count + epsilon)
    factor = jnp.minimum(1.0, clip_level / root_mean)

    for c in ma:
        c.wait_recv()
    lane = lax.broadcasted_iota(jnp.int32, (NZ, BLOCK), 1)
    for j in range(per):
        out = jnp.zeros((NZ, BLOCK), F32)
        for g in range(NY):
            rolled = pltpu.roll(max_all[g], (g - j) * nr % BLOCK, 1)
            out = jnp.where((lane >= g * nr) & (lane < g * nr + nr), rolled, out)
        scales_ref[pl.ds(j, NZ, stride=per), :] = out

    load_momentum.wait()
    for i in range(NZ):
        source = z if i == 0 else lax.rem(z + NZ - Z_NEAR[i - 1], NZ)
        for k in range(NY):
            group = y if k == 0 else lax.rem(y + NY - Y_STEPS[k - 1], NY)
            if k > 0:
                ref = gathered.at[group, source]
                send(ref, ref, gy_s.at[k - 1, i], gy_r.at[k - 1, i], y=1).wait_recv()

            where = (row_of(group), col_of(source))
            clipped = factor * gathered[group, source].astype(F32)
            after = outer_decay * momentum_v[where] + clipped
            momentum_ref[where] = after
            params_ref[where] = outer_v[where] - outer_rate * (clipped + outer_decay * after)

    for c in my + mz + ma + gz + qz + qy + qc:
        c.wait_send()
    for group in (raw, part, gy):
        for c in group.values():
            c.wait_send()


def per_device(outer_params, local_params, momentum):
    rows, cols = outer_params.shape
    nr, nc = rows // NY, cols // NZ
    vmem = pltpu.VMEM
    dma = pltpu.SemaphoreType.DMA
    return pl.pallas_call(
        kernel,
        out_shape=(
            jax.ShapeDtypeStruct((rows, cols), F32),
            jax.ShapeDtypeStruct((rows, cols), F32),
            jax.ShapeDtypeStruct((cols // BLOCK, rows), F32),
        ),
        in_specs=[pl.BlockSpec(memory_space=pl.ANY)] * 3,
        out_specs=[pl.BlockSpec(memory_space=pltpu.VMEM)] * 3,
        scratch_shapes=[
            vmem((rows, cols), F32),
            vmem((rows, cols), BF16),
            vmem((rows, cols), F32),
            vmem((NY, NZ, BLOCK), F32),
            vmem((NY - 1, NZ, BLOCK), F32),
            vmem((NZ, BLOCK), F32),
            vmem((NZ - 1, NZ, BLOCK), F32),
            vmem((NZ, BLOCK), F32),
            vmem((NY, NZ, BLOCK), F32),
            vmem((NZ, BLOCK, BLOCK), F32),
            vmem((BLOCK, BLOCK), F32),
            vmem((NY - 1, NZ, nr, nc), BF16),
            vmem((NZ - 1, nr, nc), BF16),
            vmem((nr, nc), F32),
            vmem((NZ - 1, nr, nc), BF16),
            vmem((NY, NZ, nr, nc), BF16),
            vmem((4, 8, BLOCK), F32),
            vmem((17, 8, BLOCK), F32),
            dma((2 * NY + 1,)),
            dma((3,)), dma((3,)), dma((7,)), dma((7,)), dma((3,)), dma((3,)),
            dma((3, NZ)), dma((3, NZ)), dma((7,)), dma((7,)),
            dma((7,)), dma((7,)), dma((3, NZ)), dma((3, NZ)), dma((17,)), dma((17,)),
        ],
        compiler_params=pltpu.CompilerParams(collective_id=0, has_side_effects=True),
        name="outer_step",
    )(outer_params, local_params, momentum)


def solution(mesh):
    finer = Mesh(mesh.devices.reshape([SIZES[a] for a in AXES]), AXES)
    placed = (P(SHARD, None), P(REPLICA, SHARD, None), P(SHARD, None))
    return jax.shard_map(
        per_device,
        mesh=finer,
        in_specs=placed,
        out_specs=(P(SHARD, None), P(SHARD, None), P(None, SHARD)),
        check_vma=False,
    )
```

time: 186 us -> 57 us (0.31)
  the two profiles are of different devices: /device:TPU:2 before, /device:TPU:1 now
where the time goes in v1:
time: 57 us; the launch traced here: 56.9 us
  Pallas kernels  51.1 us (90%)
  local copies, waits for them, and re-layouts  5.19 us (9%)
  between operations  0.65 us (1%)
    pallas_call x1, Pallas kernels, per_device(): pl.pallas_call(kernel, out_shape=(jax.ShapeDtypeStruct((rows, cols), F32)...  51.1 us
    unnamed x7, local copies, waits for them, and re-layouts  5.19 us

profile of v1, /device:TPU:1, one launch (start us, length us, event | category | flops | bytes accessed | tf_op | source)
XLA Modules:
  0.0 56.9 jit_solution(8570001983839917459)
XLA Ops:
  0.6 51.1 %outer_step.1 = (f32[128,4096]{1,0:T(8,128)}, f32[128,4096]{1,0:T(8,128)}, f32[32,128]{1,0:T(8,128)}) custom-call(f32[128,4096]{1,0:T(8,128)} %outer_hbm.1, bf16[1,128,4096]{2,1,0:T(8,128)(2,1)} %local_hbm.1, f32[128,4096]{1,0:T(8,128)} %momentum_hbm.1), custom_call_target="tpu_custom_call" | custom-call | tf_op jit(solution)/shard_map/outer_step/pallas_call | solution.py:311
  51.7 0.0 copy-start
  51.7 3.3 %copy.9 = f32[128,4096]{1,0:T(8,128)} copy(f32[128,4096]{1,0:T(8,128)} %get-tuple-element.6) | data formatting | bytes 4194304
  55.0 0.0 copy-done
  55.0 0.0 copy-start.1
  55.0 1.3 %copy.10 = f32[128,4096]{1,0:T(8,128)} copy(f32[128,4096]{1,0:T(8,128)S(1)} %copy-done) | data formatting | bytes 4194304
  56.3 0.0 copy-done.1
  56.3 0.6 %copy.11 = f32[32,128]{1,0:T(8,128)} copy(f32[32,128]{1,0:T(8,128)S(1)} %copy-done.1) | data formatting | bytes 32768
Async XLA Ops:
  51.7 3.3 %copy-start = (f32[128,4096]{1,0:T(8,128)S(1)}, f32[128,4096]{1,0:T(8,128)}, u32[]{:S(2)}) copy-start(f32[128,4096]{1,0:T(8,128)} %get-tuple-element.7) | copy-start | bytes 6291460
  55.0 1.3 %copy-start.1 = (f32[32,128]{1,0:T(8,128)S(1)}, f32[32,128]{1,0:T(8,128)}, u32[]{:S(2)}) copy-start(f32[32,128]{1,0:T(8,128)} %get-tuple-element.8) | copy-start | bytes 49156

commit v2 on v1

v2 whole, which is shorter than its diff:
```python
import jax
import jax.numpy as jnp
from jax import lax
from jax.experimental import pallas as pl
from jax.experimental.pallas import tpu as pltpu
from jax.sharding import Mesh
from jax.sharding import PartitionSpec as P

F32, BF16 = jnp.float32, jnp.bfloat16
MESH = pl.DeviceIdType.MESH
BLOCK = 128
AXES = ("y", "z", "x", "core")
SIZES = {"y": 4, "z": 8, "x": 4, "core": 2}
REPLICA = ("y", "z")
SHARD = ("x", "core")
NY, NZ = SIZES["y"], SIZES["z"]
WORKERS = NY * NZ

epsilon = 1e-06
clip_level = 0.5
outer_rate = 0.7
outer_decay = 0.9
grid_levels = 7.0

CURVE = (
    6.579736058540756,
    -12.987862704441794,
    12.207700561043827,
    -6.688877467338575,
    2.372163287039885,
    -0.5163244078344457,
)

Y_STEPS = (2, 1, 3)
Z_FAR = (4, 3, 5, 2, 6, 1, 7)
Z_NEAR = (1, 7, 2, 6, 3, 5, 4)
CELL = tuple((a, b) for a in range(4) for b in range(2) if (a, b) != (0, 0))


def curve(r):
    t = r * r
    p = CURVE[-1]
    for c in CURVE[-2::-1]:
        p = p * t + c
    return (r * t) * p


def smooth_round(v):
    whole = jnp.round(v)
    return whole + curve(curve(v - whole))


def eighth_power(s):
    t = s * s
    return (s * jnp.abs(s)) * t * (t * t)


def eighth_root(c):
    c = c.astype(F32)
    size = jnp.exp(0.125 * jnp.log(jnp.maximum(jnp.abs(c), 1e-37)))
    return jnp.where(c < 0.0, -size, size)


def kernel(
    outer_hbm, local_hbm, momentum_hbm, params_ref, momentum_ref, scales_ref,
    outer_v, local_v, momentum_v, maxima, maxima_y, max_own, maxima_z, max_all,
    inverse, spread, raw_y, partial, total, parts_z, gathered, squares, squares_in,
    load_sem, my_s, my_r, mz_s, mz_r, ma_s, ma_r, raw_s, raw_r, part_s, part_r,
    gz_s, gz_r, gy_s, gy_r, sq_s, sq_r,
):
    y, z = lax.axis_index("y"), lax.axis_index("z")
    x, core = lax.axis_index("x"), lax.axis_index("core")
    at = {"y": y, "z": z, "x": x, "core": core}
    rows, cols = outer_v.shape
    nr, nc = rows // NY, cols // NZ
    per = nc // BLOCK
    nb = cols // BLOCK
    entry_count = rows * cols * SIZES["x"] * SIZES["core"]
    lane = lax.broadcasted_iota(jnp.int32, (8, BLOCK), 1)

    def peer(**steps):
        return {k: lax.rem(at[k] + s, SIZES[k]) for k, s in steps.items()}

    def send(src, dst, ss, rs, **steps):
        return pltpu.make_async_remote_copy(
            src_ref=src, dst_ref=dst, send_sem=ss, recv_sem=rs,
            device_id=peer(**steps), device_id_type=MESH,
        )

    def row_of(g):
        return pl.ds(pl.multiple_of(g * nr, nr), nr)

    def col_of(g):
        return pl.ds(pl.multiple_of(g * nc, nc), nc)

    def aligned(n):
        return pl.ds(pl.multiple_of(n * BLOCK, BLOCK), BLOCK)

    barrier = pltpu.get_barrier_semaphore()
    friends = (
        [dict(y=s) for s in range(1, NY)]
        + [dict(z=s) for s in range(1, NZ)]
        + [dict(x=a, core=b) for a, b in CELL]
    )
    for f in friends:
        pl.semaphore_signal(barrier, inc=1, device_id=peer(**f), device_id_type=MESH)

    load_local = pltpu.make_async_copy(local_hbm.at[0], local_v, load_sem.at[NY])
    load_momentum = pltpu.make_async_copy(momentum_hbm, momentum_v, load_sem.at[NY + 1])
    load_outer = [
        pltpu.make_async_copy(
            outer_hbm.at[pl.ds(g * nr, nr)], outer_v.at[pl.ds(g * nr, nr)], load_sem.at[g]
        )
        for g in range(NY)
    ]
    for c in [load_local, *load_outer, load_momentum]:
        c.start()
    load_local.wait()
    pl.semaphore_wait(barrier, len(friends))

    order = (4, 3, 5, 2, 6, 1, 7, 0)
    pieces = [lax.rem(z + o, NZ) for o in order]
    raw = {}

    def send_raw(i):
        for k, s in enumerate(Y_STEPS):
            raw[i, k] = send(
                local_v.at[row_of(lax.rem(y + s, NY)), col_of(pieces[i])],
                raw_y.at[k, i], raw_s.at[k, i], raw_r.at[k, i], y=s,
            )
            raw[i, k].start()

    send_raw(0)
    send_raw(1)

    for g in range(NY):
        load_outer[g].wait()

        def block_max(b, acc, g=g):
            out = acc
            for r in range(nr // 8):
                where = (pl.ds(g * nr + r * 8, 8), aligned(b))
                deltas = outer_v[where] - local_v[where].astype(F32)
                most = jnp.max(jnp.abs(deltas), axis=1, keepdims=True)
                out = jnp.where(lane == r * nb + b, most, out)
            return out

        maxima[g] = lax.fori_loop(0, nb, block_max, jnp.zeros((8, BLOCK), F32), unroll=16)

    my = [
        send(maxima.at[lax.rem(y + s, NY)], maxima_y.at[i], my_s.at[i], my_r.at[i], y=s)
        for i, s in enumerate(Y_STEPS)
    ]
    for c in my:
        c.start()
    for i in range(2, NZ):
        send_raw(i)
    for c in my:
        c.wait_recv()
    m = maxima[y]
    for i in range(len(Y_STEPS)):
        m = jnp.maximum(m, maxima_y[i])
    max_own[...] = m
    mz = [
        send(max_own, maxima_z.at[i], mz_s.at[i], mz_r.at[i], z=s) for i, s in enumerate(Z_FAR)
    ]
    for c in mz:
        c.start()
    for c in mz:
        c.wait_recv()
    m = max_own[...]
    for i in range(len(Z_FAR)):
        m = jnp.maximum(m, maxima_z[i])
    max_all[y] = m
    ma = [
        send(max_all.at[y], max_all.at[y], ma_s.at[i], ma_r.at[i], y=s)
        for i, s in enumerate(Y_STEPS)
    ]
    for c in ma:
        c.start()

    scale = m + epsilon
    inverse_scale = grid_levels / scale
    for b in range(nb):
        for r in range(nr // 8):
            n = r * nb + b
            inverse[b, pl.ds(r * 8, 8), :] = jnp.broadcast_to(
                inverse_scale[:, n : n + 1], (8, BLOCK)
            )

    part = {}
    for i in range(NZ):
        p = pieces[i]
        for k in range(len(Y_STEPS)):
            raw[i, k].wait_recv()

        def encode(j, _, i=i, p=p):
            lanes = aligned(j)
            columns = aligned(p * per + j)
            o = outer_v[row_of(y), columns]
            inv = inverse[p * per + j]
            acc = jnp.zeros((nr, BLOCK), F32)
            for w in range(NY):
                local = local_v[row_of(y), columns] if w == 0 else raw_y[w - 1, i, :, lanes]
                v = (o - local.astype(F32)) * inv
                acc += smooth_round(v).astype(BF16).astype(F32)
            if i < NZ - 1:
                partial[i, :, lanes] = eighth_power(acc).astype(BF16)
            else:
                total[:, lanes] = acc
            return 0

        lax.fori_loop(0, per, encode, 0)
        if i < NZ - 1:
            part[i] = send(
                partial.at[i], parts_z.at[i], part_s.at[i], part_r.at[i], z=order[i]
            )
            part[i].start()

    for i in range(NZ - 1):
        part[i].wait_recv()

    sq = jnp.zeros((8, BLOCK), F32)
    for j in range(per):
        lanes = pl.ds(j * BLOCK, BLOCK)
        acc = total[:, lanes]
        for i in range(NZ - 1):
            acc += eighth_root(parts_z[i, :, lanes])
        gathered[y, z, :, lanes] = eighth_power(acc).astype(BF16)
        g = acc / inverse[z * per + j] * (1.0 / WORKERS)
        g2 = g * g
        for r in range(nr // 8):
            sq += g2[r * 8 : r * 8 + 8]
    squares[0] = sq

    qc = [
        send(squares.at[0], squares_in.at[i], sq_s.at[i], sq_r.at[i], x=a, core=b)
        for i, (a, b) in enumerate(CELL)
    ]
    gz = [
        send(gathered.at[y, z], gathered.at[y, z], gz_s.at[i], gz_r.at[i], z=s)
        for i, s in enumerate(Z_NEAR)
    ]
    gy = {}

    def spread_y(i, source):
        for k, s in enumerate(Y_STEPS):
            ref = gathered.at[y, source]
            gy[i, k] = send(ref, ref, gy_s.at[k, i], gy_r.at[k, i], y=s)
            gy[i, k].start()

    def add_up(slot, first, copies):
        for c in copies:
            c.wait_recv()
        acc = squares[slot]
        for i in range(len(copies)):
            acc += squares_in[first + i]
        squares[slot + 1] = acc

    def pass_on(i):
        source = lax.rem(z + NZ - Z_NEAR[i], NZ)
        ref = gathered.at[y, source]
        send(ref, ref, gz_s.at[i], gz_r.at[i], z=Z_NEAR[i]).wait_recv()
        spread_y(i + 1, source)

    for c in gz:
        c.start()
    for c in qc:
        c.start()
    spread_y(0, z)

    for c in ma:
        c.wait_recv()
    for g in range(NY):
        group_scale = (max_all[g] + epsilon) * (1.0 / (grid_levels * WORKERS))
        for b in range(nb):
            for r in range(nr // 8):
                n = r * nb + b
                spread[b, pl.ds(g * nr + r * 8, 8), :] = jnp.broadcast_to(
                    group_scale[:, n : n + 1], (8, BLOCK)
                )
        if g == 0:
            pass_on(0)
    add_up(0, 0, qc)
    qy = [
        send(squares.at[1], squares_in.at[7 + i], sq_s.at[7 + i], sq_r.at[7 + i], y=s)
        for i, s in enumerate(Y_STEPS)
    ]
    for q in qy:
        q.start()
    pass_on(1)
    pass_on(2)
    pass_on(3)
    add_up(1, 7, qy)
    qz = [
        send(squares.at[2], squares_in.at[10 + i], sq_s.at[10 + i], sq_r.at[10 + i], z=s)
        for i, s in enumerate(Z_NEAR)
    ]
    for q in qz:
        q.start()
    for i in range(4, NZ - 1):
        pass_on(i)

    stack = []
    for g in range(NY):
        for r in range(nr // 8):
            turned = max_all[g] if r == 0 else pltpu.roll(max_all[g], BLOCK - r * nb, 1)
            stack.append(turned)
    scales_ref[...] = jnp.concatenate(stack, axis=0).T[:nb]

    load_momentum.wait()
    add_up(2, 10, qz)
    square_total = jnp.sum(squares[3], axis=(0, 1), keepdims=True)
    root_mean = jnp.sqrt(square_total / entry_count + epsilon)
    factor = jnp.minimum(1.0, clip_level / root_mean)

    for i in range(NZ):
        source = z if i == 0 else lax.rem(z + NZ - Z_NEAR[i - 1], NZ)
        for k in range(NY):
            group = y if k == 0 else lax.rem(y + NY - Y_STEPS[k - 1], NY)
            if k > 0:
                ref = gathered.at[group, source]
                send(ref, ref, gy_s.at[k - 1, i], gy_r.at[k - 1, i], y=1).wait_recv()

            def outer_step(j, _, source=source, group=group):
                where = (row_of(group), aligned(source * per + j))
                sums = eighth_root(gathered[group, source, :, aligned(j)])
                clipped = sums * spread[source * per + j, row_of(group)] * factor
                after = outer_decay * momentum_v[where] + clipped
                momentum_ref[where] = after
                params_ref[where] = outer_v[where] - outer_rate * (clipped + outer_decay * after)
                return 0

            lax.fori_loop(0, per, outer_step, 0, unroll=True)

    for c in my + mz + ma + gz + qz + qy + qc:
        c.wait_send()
    for copies in (raw, part, gy):
        for c in copies.values():
            c.wait_send()


def per_device(outer_params, local_params, momentum):
    rows, cols = outer_params.shape
    nr, nc = rows // NY, cols // NZ
    vmem = pltpu.VMEM
    dma = pltpu.SemaphoreType.DMA
    return pl.pallas_call(
        kernel,
        out_shape=(
            jax.ShapeDtypeStruct((rows, cols), F32),
            jax.ShapeDtypeStruct((rows, cols), F32),
            jax.ShapeDtypeStruct((cols // BLOCK, rows), F32),
        ),
        in_specs=[pl.BlockSpec(memory_space=pltpu.HBM)] * 3,
        out_specs=[pl.BlockSpec(memory_space=pltpu.VMEM)] * 3,
        scratch_shapes=[
            vmem((rows, cols), F32),
            vmem((rows, cols), BF16),
            vmem((rows, cols), F32),
            vmem((NY, 8, BLOCK), F32),
            vmem((NY - 1, 8, BLOCK), F32),
            vmem((8, BLOCK), F32),
            vmem((NZ - 1, 8, BLOCK), F32),
            vmem((NY, 8, BLOCK), F32),
            vmem((cols // BLOCK, nr, BLOCK), F32),
            vmem((cols // BLOCK, rows, BLOCK), F32),
            vmem((NY - 1, NZ, nr, nc), BF16),
            vmem((NZ - 1, nr, nc), BF16),
            vmem((nr, nc), F32),
            vmem((NZ - 1, nr, nc), BF16),
            vmem((NY, NZ, nr, nc), BF16),
            vmem((4, 8, BLOCK), F32),
            vmem((17, 8, BLOCK), F32),
            dma((NY + 2,)),
            dma((3,)), dma((3,)), dma((7,)), dma((7,)), dma((3,)), dma((3,)),
            dma((3, NZ)), dma((3, NZ)), dma((7,)), dma((7,)),
            dma((7,)), dma((7,)), dma((3, NZ)), dma((3, NZ)), dma((17,)), dma((17,)),
        ],
        compiler_params=pltpu.CompilerParams(
            collective_id=0, has_side_effects=True, vmem_limit_bytes=32 * 1024 * 1024
        ),
        name="outer_step",
    )(*[pltpu.with_memory_space_constraint(a, pltpu.HBM) for a in (outer_params, local_params, momentum)])


def solution(mesh):
    finer = Mesh(mesh.devices.reshape([SIZES[a] for a in AXES]), AXES)
    placed = (P(SHARD, None), P(REPLICA, SHARD, None), P(SHARD, None))
    return jax.shard_map(
        per_device,
        mesh=finer,
        in_specs=placed,
        out_specs=(P(SHARD, None), P(SHARD, None), P(None, SHARD)),
        check_vma=False,
    )
```

time: 57 us -> 50.1 us (0.88)
  Pallas kernels: 51.1 us -> 46.2 us
  local copies, waits for them, and re-layouts: 5.19 us -> 3.24 us
    pallas_call x1, Pallas kernels: 51.1 us -> 46.2 us  [per_device(): pl.pallas_call(kernel, out_shape=(jax.ShapeDtypeStruct((rows, cols), F32)...]
    unnamed x7 -> x3, local copies, waits for them, and re-layouts: 5.19 us -> 3.24 us
where the time goes in v2:
time: 50.1 us; the launch traced here: 50 us
  Pallas kernels  46.2 us (92%)
  local copies, waits for them, and re-layouts  3.24 us (6%)
  between operations  0.64 us (1%)
    pallas_call x1, Pallas kernels, per_device(): pl.pallas_call(kernel, out_shape=(jax.ShapeDtypeStruct((rows, cols), F32)...  46.2 us
    unnamed x3, local copies, waits for them, and re-layouts  3.24 us

profile of v2, /device:TPU:1, one launch (start us, length us, event | category | flops | bytes accessed | tf_op | source)
XLA Modules:
  0.0 50.0 jit_solution(15230731086348614145)
XLA Ops:
  0.6 46.2 %outer_step.1 = (f32[128,4096]{1,0:T(8,128)S(1)}, f32[128,4096]{1,0:T(8,128)S(1)}, f32[32,128]{1,0:T(8,128)S(1)}) custom-call(f32[128,4096]{1,0:T(8,128)} %outer_hbm.1, bf16[1,128,4096]{2,1,0:T(8,128)(2,1)} %local_hbm.1, f32[128,4096]{1,0:T(8,128)} %momentum_hbm.1), custom_call_target="tpu_custom_call" | custom-call | tf_op jit(solution)/shard_map/outer_step/pallas_call | solution.py:348
  46.8 1.3 %copy.9 = f32[128,4096]{1,0:T(8,128)} copy(f32[128,4096]{1,0:T(8,128)S(1)} %get-tuple-element.6) | data formatting | bytes 4194304
  48.1 1.3 %copy.10 = f32[128,4096]{1,0:T(8,128)} copy(f32[128,4096]{1,0:T(8,128)S(1)} %get-tuple-element.7) | data formatting | bytes 4194304
  49.4 0.6 %copy.11 = f32[32,128]{1,0:T(8,128)} copy(f32[32,128]{1,0:T(8,128)S(1)} %get-tuple-element.8) | data formatting | bytes 32768

commit v3 on v2

v3 whole, which is shorter than its diff:
```python
import jax
import jax.numpy as jnp
from jax import lax
from jax.experimental import pallas as pl
from jax.experimental.pallas import tpu as pltpu
from jax.sharding import Mesh
from jax.sharding import PartitionSpec as P

F32, BF16 = jnp.float32, jnp.bfloat16
MESH = pl.DeviceIdType.MESH
BLOCK = 128
AXES = ("y", "z", "x", "core")
SIZES = {"y": 4, "z": 8, "x": 4, "core": 2}
REPLICA = ("y", "z")
SHARD = ("x", "core")
NY, NZ = SIZES["y"], SIZES["z"]
WORKERS = NY * NZ

epsilon = 1e-06
clip_level = 0.5
outer_rate = 0.7
outer_decay = 0.9
grid_levels = 7.0

CURVE = (
    6.579736058540756,
    -12.987862704441794,
    12.207700561043827,
    -6.688877467338575,
    2.372163287039885,
    -0.5163244078344457,
)

Y_STEPS = (2, 1, 3)
Z_FAR = (4, 3, 5, 2, 6, 1, 7)
Z_NEAR = (1, 7, 2, 6, 3, 5, 4)
CELL = tuple((a, b) for a in range(4) for b in range(2) if (a, b) != (0, 0))


def curve(r):
    t = r * r
    p = CURVE[-1]
    for c in CURVE[-2::-1]:
        p = p * t + c
    return (r * t) * p


def smooth_round(v):
    whole = jnp.round(v)
    return whole + curve(curve(v - whole))


def eighth_power(s):
    t = s * s
    return (s * jnp.abs(s)) * t * (t * t)


def eighth_root(c):
    c = c.astype(F32)
    size = jnp.exp(0.125 * jnp.log(jnp.maximum(jnp.abs(c), 1e-37)))
    return jnp.where(c < 0.0, -size, size)


def kernel(
    outer_hbm, local_hbm, momentum_hbm, gradient_ref, factor_ref, scales_ref, outer_v, momentum_v,
    local_v, maxima, maxima_y, max_own, maxima_z, max_all,
    inverse, inverse_z, spread, raw_y, raw_z, partial, partial_y, total, parts_z, parts_y, gathered,
    squares, squares_in, load_sem, one_s, one_r, raw_r, gz_r, gy_r, gh_r,
):
    y, z = lax.axis_index("y"), lax.axis_index("z")
    x, core = lax.axis_index("x"), lax.axis_index("core")
    at = {"y": y, "z": z, "x": x, "core": core}
    rows, cols = outer_v.shape
    nr, nc = rows // NY, cols // NZ
    per = nc // BLOCK
    near = per - 1
    nb = cols // BLOCK
    entry_count = rows * cols * SIZES["x"] * SIZES["core"]
    lane = lax.broadcasted_iota(jnp.int32, (8, BLOCK), 1)
    MY, MZ, MA, RY, RZ, PZ, PY, GZ, GO, GY, GH, QC, QY, QZ = range(14)

    def peer(**steps):
        return {k: lax.rem(at[k] + s, SIZES[k]) for k, s in steps.items()}

    def send(src, dst, ss, rs, **steps):
        pltpu.make_async_remote_copy(
            src_ref=src, dst_ref=dst, send_sem=ss, recv_sem=rs,
            device_id=peer(**steps), device_id_type=MESH,
        ).start()

    def all_of(ref, ss, rs):
        return pltpu.make_async_remote_copy(
            src_ref=ref, dst_ref=ref, send_sem=ss, recv_sem=rs,
            device_id=peer(y=1), device_id_type=MESH,
        )

    def landed(ref, sem):
        all_of(ref, one_s.at[0], sem).wait_recv()

    def row_of(g):
        return pl.ds(pl.multiple_of(g * nr, nr), nr)

    def aligned(n, count=1):
        return pl.ds(pl.multiple_of(n * BLOCK, BLOCK), count * BLOCK)

    barrier = pltpu.get_barrier_semaphore()
    friends = (
        [dict(y=s) for s in range(1, NY)]
        + [dict(z=s) for s in range(1, NZ)]
        + [dict(x=a, core=b) for a, b in CELL]
    )
    for f in friends:
        pl.semaphore_signal(barrier, inc=1, device_id=peer(**f), device_id_type=MESH)

    load_momentum = pltpu.make_async_copy(momentum_hbm, momentum_v, load_sem.at[2, 0])
    loads = [
        pltpu.make_async_copy(src.at[pl.ds(g * nr, nr)], dst.at[pl.ds(g * nr, nr)], load_sem.at[k, g])
        for g in range(NY)
        for k, (src, dst) in enumerate(((local_hbm.at[0], local_v), (outer_hbm, outer_v)))
    ]
    for c in [*loads, load_momentum]:
        c.start()

    lasts = jnp.zeros((8, BLOCK), F32)
    for g in range(NY):
        loads[2 * g].wait()
        loads[2 * g + 1].wait()

        def block_max(p, acc, g=g):
            out, lasts = acc
            for j in range(per):
                for r in range(nr // 8):
                    where = (pl.ds(g * nr + r * 8, 8), aligned(p * per + j))
                    deltas = outer_v[where] - local_v[where].astype(F32)
                    most = jnp.max(jnp.abs(deltas), axis=1, keepdims=True)
                    out = jnp.where(lane == r * nb + p * per + j, most, out)
                    if j == near:
                        lasts = jnp.where(lane == p * (rows // 8) + g * (nr // 8) + r, most, lasts)
            return out, lasts

        maxima[g], lasts = lax.fori_loop(
            0, NZ, block_max, (jnp.zeros((8, BLOCK), F32), lasts), unroll=4
        )
    maxima[NY] = lasts

    pl.semaphore_wait(barrier, len(friends))

    order = (4, 3, 5, 2, 6, 1, 7, 0)
    pieces = [lax.rem(z + o, NZ) for o in order]

    def send_raw_y(i):
        for k, s in enumerate(Y_STEPS):
            send(
                local_v.at[row_of(lax.rem(y + s, NY)), aligned(pieces[i] * per, near)],
                raw_y.at[k, i], one_s.at[RY], raw_r.at[i], y=s,
            )

    def send_raw_z(i):
        s = Z_FAR[i]
        send(
            local_v.at[:, aligned(lax.rem(z + s, NZ) * per + near)],
            raw_z.at[i], one_s.at[RZ], one_r.at[RZ], z=s,
        )

    for i, s in enumerate(Y_STEPS):
        send(maxima.at[lax.rem(y + s, NY)], maxima_y.at[i, 0], one_s.at[MY], one_r.at[MY], y=s)
        send(maxima.at[NY], maxima_y.at[i, 1], one_s.at[MY], one_r.at[MY], y=s)
    for i in range(NZ):
        send_raw_y(i)
        if i < 2:
            send_raw_z(i)
    landed(maxima_y, one_r.at[MY])
    for k, row in enumerate((y, NY)):
        m = maxima[row]
        for i in range(len(Y_STEPS)):
            m = jnp.maximum(m, maxima_y[i, k])
        max_own[k] = m
    for i, s in enumerate(Z_FAR):
        send(max_own, maxima_z.at[i], one_s.at[MZ], one_r.at[MZ], z=s)
    for i in range(2, NZ - 1):
        send_raw_z(i)
    landed(maxima_z, one_r.at[MZ])
    m, lasts = max_own[0], max_own[1]
    for i in range(len(Z_FAR)):
        m = jnp.maximum(m, maxima_z[i, 0])
        lasts = jnp.maximum(lasts, maxima_z[i, 1])
    max_all[y] = m
    for s in Y_STEPS:
        send(max_all.at[y], max_all.at[y], one_s.at[MA], one_r.at[MA], y=s)

    inverse_scale = grid_levels / (m + epsilon)
    for b in range(nb):
        for r in range(nr // 8):
            n = r * nb + b
            inverse[b, pl.ds(r * 8, 8), :] = jnp.broadcast_to(
                inverse_scale[:, n : n + 1], (8, BLOCK)
            )

    def encoded(o, local, inv):
        v = (o - local.astype(F32)) * inv
        return smooth_round(v).astype(BF16).astype(F32)

    def along_y(i):
        p = pieces[i]
        landed(raw_y.at[:, i], raw_r.at[i])

        def encode(j, _):
            lanes = aligned(j)
            columns = aligned(p * per + j)
            o = outer_v[row_of(y), columns]
            inv = inverse[p * per + j]
            acc = encoded(o, local_v[row_of(y), columns], inv)
            for k in range(len(Y_STEPS)):
                acc += encoded(o, raw_y[k, i, :, lanes], inv)
            if i < NZ - 1:
                partial[i, :, lanes] = eighth_power(acc).astype(BF16)
            else:
                total[:, lanes] = acc
            return 0

        lax.fori_loop(0, near, encode, 0)
        if i < NZ - 1:
            send(partial.at[i], parts_z.at[i], one_s.at[PZ], one_r.at[PZ], z=order[i])

    def along_z():
        landed(raw_z, one_r.at[RZ])
        last = z * per + near
        turned = pltpu.roll(grid_levels / (lasts + epsilon), BLOCK - z * (rows // 8), 1)
        for r in range(rows // 8):
            inverse_z[pl.ds(r * 8, 8), :] = jnp.broadcast_to(turned[:, r : r + 1], (8, BLOCK))

        def encode(g, _):
            inv = inverse_z[row_of(g), :]
            o = outer_v[row_of(g), aligned(last)]
            acc = encoded(o, local_v[row_of(g), aligned(last)], inv)
            for k in range(NZ - 1):
                acc += encoded(o, raw_z[k, row_of(g), :], inv)
            partial_y[g] = eighth_power(acc).astype(BF16)

            @pl.when(g == y)
            def _():
                total[:, pl.ds(near * BLOCK, BLOCK)] = acc

            return 0

        lax.fori_loop(0, NY, encode, 0)
        for k, s in enumerate(Y_STEPS):
            send(partial_y.at[lax.rem(y + s, NY)], parts_y.at[k], one_s.at[PY], one_r.at[PY], y=s)

    for i in range(5):
        along_y(i)
    along_z()
    for i in range(5, NZ):
        along_y(i)
    landed(parts_z, one_r.at[PZ])
    landed(parts_y, one_r.at[PY])

    sq = jnp.zeros((8, BLOCK), F32)
    for j in range(per):
        lanes = pl.ds(j * BLOCK, BLOCK)
        acc = total[:, lanes]
        if j < near:
            for i in range(NZ - 1):
                acc += eighth_root(parts_z[i, :, lanes])
        else:
            for i in range(NY - 1):
                acc += eighth_root(parts_y[i])
        gathered[y, z, j] = eighth_power(acc).astype(BF16)
        g = acc / inverse[z * per + j] * (1.0 / WORKERS)
        g2 = g * g
        for r in range(nr // 8):
            sq += g2[r * 8 : r * 8 + 8]
    squares[0] = sq

    most = pl.ds(0, near)

    def pass_on(i):
        source = lax.rem(z + NZ - Z_NEAR[i], NZ)
        ref = gathered.at[y, source, most]
        landed(ref, gz_r.at[i])
        for s in Y_STEPS:
            send(ref, ref, one_s.at[GY], gy_r.at[i], y=s)

    def pass_last(i):
        ref = gathered.at[:, z, near]
        send(ref, ref, one_s.at[GH], gh_r.at[i], z=Z_FAR[i])

    def add_up(slot, first, count, sem):
        landed(squares_in.at[pl.ds(first, count)], sem)
        acc = squares[slot]
        for i in range(count):
            acc += squares_in[first + i]
        squares[slot + 1] = acc

    for i, s in enumerate(Z_NEAR):
        send(squares.at[0], squares_in.at[i], one_s.at[QZ], one_r.at[QZ], z=s)
    ref = gathered.at[y, z, most]
    for i, s in enumerate(Z_NEAR):
        send(ref, ref, one_s.at[GZ], gz_r.at[i], z=s)
    ref = gathered.at[y, z]
    for s in Y_STEPS:
        send(ref, ref, one_s.at[GO], one_r.at[GO], y=s)

    def spread_scale(g):
        group_scale = (max_all[g] + epsilon) * (1.0 / (grid_levels * WORKERS))
        for b in range(nb):
            for r in range(nr // 8):
                n = r * nb + b
                spread[b, pl.ds(g * nr + r * 8, 8), :] = jnp.broadcast_to(
                    group_scale[:, n : n + 1], (8, BLOCK)
                )

    landed(maxima_y.at[:, 0], one_r.at[MA])
    spread_scale(0)
    spread_scale(1)
    pass_on(0)
    pass_on(1)
    landed(raw_z.at[pl.ds(0, NY - 1)], one_r.at[GO])
    for i in range(NZ - 1):
        pass_last(i)
    add_up(0, 0, 7, one_r.at[QZ])
    for i, s in enumerate(Y_STEPS):
        send(squares.at[1], squares_in.at[7 + i], one_s.at[QY], one_r.at[QY], y=s)
    pass_on(2)
    spread_scale(2)
    pass_on(3)
    spread_scale(3)
    pass_on(4)
    add_up(1, 7, 3, one_r.at[QY])
    for i, (a, b) in enumerate(CELL):
        send(squares.at[2], squares_in.at[10 + i], one_s.at[QC], one_r.at[QC], x=a, core=b)
    pass_on(5)
    pass_on(6)

    stack = []
    for g in range(NY):
        for r in range(nr // 8):
            turned = max_all[g] if r == 0 else pltpu.roll(max_all[g], BLOCK - r * nb, 1)
            stack.append(turned)
    scales_ref[...] = jnp.concatenate(stack, axis=0).T[:nb]

    for i in range(NZ):
        source = z if i == 0 else lax.rem(z + NZ - Z_NEAR[i - 1], NZ)
        if i > 0:
            landed(raw_y.at[:, 0], gy_r.at[i - 1])
            landed(gathered.at[:, source, near], gh_r.at[Z_FAR.index(Z_NEAR[i - 1])])

        def decode(group, _, source=source):
            for j in range(per):
                sums = eighth_root(gathered[group, source, j])
                gradient_ref[row_of(group), aligned(source * per + j)] = (
                    sums * spread[source * per + j, row_of(group)]
                )
            return 0

        lax.fori_loop(0, NY, decode, 0, unroll=2)

    load_momentum.wait()
    add_up(2, 10, 7, one_r.at[QC])
    square_total = jnp.sum(squares[3], axis=(0, 1), keepdims=True)
    root_mean = jnp.sqrt(square_total / entry_count + epsilon)
    factor_ref[...] = jnp.broadcast_to(jnp.minimum(1.0, clip_level / root_mean), (8, BLOCK))

    for ref, n in (
        (maxima_y, MY), (maxima_z, MZ), (maxima_y.at[:, 0], MA), (raw_y, RY), (raw_z, RZ), (parts_z, PZ),
        (parts_y, PY), (parts_z, GZ), (raw_z.at[pl.ds(0, NY - 1)], GO),
        (raw_y.at[:, pl.ds(0, NZ - 1)], GY), (raw_z, GH), (squares_in.at[pl.ds(0, 7)], QC),
        (squares_in.at[pl.ds(7, 3)], QY), (squares_in.at[pl.ds(10, 7)], QZ),
    ):
        all_of(ref, one_s.at[n], one_r.at[n]).wait_send()


def outer_step(
    gradient_ref, factor_ref, scales_ref, outer_ref, momentum_ref,
    params_hbm, momentum_hbm, scales_hbm, params_v, momentum_v, sem,
):
    parts, part = params_v.shape[0], params_v.shape[1]
    copies = [pltpu.make_async_copy(scales_ref, scales_hbm, sem.at[2 * parts])]
    copies[0].start()
    factor = factor_ref[0:1, 0:1]
    for i in range(parts):
        where = pl.ds(i * part, part)
        clipped = factor * gradient_ref[where]
        after = outer_decay * momentum_ref[where] + clipped
        momentum_v[i] = after
        params_v[i] = outer_ref[where] - outer_rate * (clipped + outer_decay * after)
        for k, (src, dst) in enumerate(((params_v, params_hbm), (momentum_v, momentum_hbm))):
            copies.append(pltpu.make_async_copy(src.at[i], dst.at[where], sem.at[2 * i + k]))
            copies[-1].start()
    for c in copies:
        c.wait()


def per_device(outer_params, local_params, momentum):
    rows, cols = outer_params.shape
    nr, nc = rows // NY, cols // NZ
    vmem = pltpu.VMEM
    dma = pltpu.SemaphoreType.DMA
    outs = pl.pallas_call(
        kernel,
        out_shape=(
            jax.ShapeDtypeStruct((rows, cols), F32),
            jax.ShapeDtypeStruct((8, BLOCK), F32),
            jax.ShapeDtypeStruct((cols // BLOCK, rows), F32),
            jax.ShapeDtypeStruct((rows, cols), F32),
            jax.ShapeDtypeStruct((rows, cols), F32),
        ),
        in_specs=[pl.BlockSpec(memory_space=pltpu.HBM)] * 3,
        out_specs=[pl.BlockSpec(memory_space=pltpu.VMEM)] * 5,
        scratch_shapes=[
            vmem((rows, cols), BF16),
            vmem((NY + 1, 8, BLOCK), F32),
            vmem((NY - 1, 2, 8, BLOCK), F32),
            vmem((2, 8, BLOCK), F32),
            vmem((NZ - 1, 2, 8, BLOCK), F32),
            vmem((NY, 8, BLOCK), F32),
            vmem((cols // BLOCK, nr, BLOCK), F32),
            vmem((rows, BLOCK), F32),
            vmem((cols // BLOCK, rows, BLOCK), F32),
            vmem((NY - 1, NZ, nr, nc - BLOCK), BF16),
            vmem((NZ - 1, rows, BLOCK), BF16),
            vmem((NZ - 1, nr, nc - BLOCK), BF16),
            vmem((NY, nr, BLOCK), BF16),
            vmem((nr, nc), F32),
            vmem((NZ - 1, nr, nc - BLOCK), BF16),
            vmem((NY - 1, nr, BLOCK), BF16),
            vmem((NY, NZ, nc // BLOCK, nr, BLOCK), BF16),
            vmem((4, 8, BLOCK), F32),
            vmem((17, 8, BLOCK), F32),
            dma((3, NY)), dma((14,)), dma((14,)),
            dma((NZ,)), dma((NZ - 1,)), dma((NZ - 1,)), dma((NZ - 1,)),
        ],
        compiler_params=pltpu.CompilerParams(
            collective_id=0, has_side_effects=True, vmem_limit_bytes=32 * 1024 * 1024
        ),
        name="synchronise",
    )(*[pltpu.with_memory_space_constraint(a, pltpu.HBM) for a in (outer_params, local_params, momentum)])


    parts = 8
    return pl.pallas_call(
        outer_step,
        out_shape=[
            jax.ShapeDtypeStruct((rows, cols), F32),
            jax.ShapeDtypeStruct((rows, cols), F32),
            jax.ShapeDtypeStruct((cols // BLOCK, rows), F32),
        ],
        in_specs=[pl.BlockSpec(memory_space=pltpu.VMEM)] * 5,
        out_specs=[pl.BlockSpec(memory_space=pltpu.HBM)] * 3,
        scratch_shapes=[
            vmem((parts, rows // parts, cols), F32),
            vmem((parts, rows // parts, cols), F32),
            dma((2 * parts + 1,)),
        ],
        compiler_params=pltpu.CompilerParams(vmem_limit_bytes=8 * 1024 * 1024),
        name="outer_step",
    )(*outs)


def solution(mesh):
    finer = Mesh(mesh.devices.reshape([SIZES[a] for a in AXES]), AXES)
    placed = (P(SHARD, None), P(REPLICA, SHARD, None), P(SHARD, None))
    return jax.shard_map(
        per_device,
        mesh=finer,
        in_specs=placed,
        out_specs=(P(SHARD, None), P(SHARD, None), P(None, SHARD)),
        check_vma=False,
    )
```

time: 50.1 us -> 44.9 us (0.90)
  local copies, waits for them, and re-layouts: 3.24 us -> 0 us
  Pallas kernels: 46.2 us -> 44.1 us
    pallas_call x1, Pallas kernels: 46.2 us -> 41.9 us  [per_device(): pl.pallas_call(kernel, out_shape=(jax.ShapeDtypeStruct((rows, cols), F32)...]
    unnamed x3 -> x0, local copies, waits for them, and re-layouts: 3.24 us -> none
    pallas_call x0 -> x1, Pallas kernels: none -> 2.28 us  [per_device(): pl.pallas_call(outer_step, out_shape=[jax.ShapeDtypeStruct((rows, cols),...]
where the time goes in v3:
time: 44.9 us; the launch traced here: 44.8 us
  Pallas kernels  44.1 us (98%)
  between operations  0.64 us (1%)
    pallas_call x1, Pallas kernels, per_device(): pl.pallas_call(kernel, out_shape=(jax.ShapeDtypeStruct((rows, cols), F32)...  41.9 us
    pallas_call x1, Pallas kernels, per_device(): pl.pallas_call(outer_step, out_shape=[jax.ShapeDtypeStruct((rows, cols),...  2.28 us

profile of v3, /device:TPU:1, one launch (start us, length us, event | category | flops | bytes accessed | tf_op | source)
XLA Modules:
  0.0 44.8 jit_solution(7427130992071129463)
XLA Ops:
  0.6 41.9 %synchronise.1 = (f32[128,4096]{1,0:T(8,128)S(1)}, f32[8,128]{1,0:T(8,128)S(1)}, f32[32,128]{1,0:T(8,128)S(1)}, f32[128,4096]{1,0:T(8,128)S(1)}, f32[128,4096]{1,0:T(8,128)S(1)}) custom-call(f32[128,4096]{1,0:T(8,128)} %outer_hbm.1, bf16[1,128,4096]{2,1,0:T(8,128)(2,1)} %local_hbm.1, f32[128,4096]{1,0:T(8,128)} %momentum_hbm.1), custom_call_target="tpu_custom_call" | custom-call | tf_op jit(solution)/shard_map/synchronise/pallas_call | solution.py:399
  42.5 2.3 %outer_step.1 = (f32[128,4096]{1,0:T(8,128)}, f32[128,4096]{1,0:T(8,128)}, f32[32,128]{1,0:T(8,128)}) custom-call(f32[128,4096]{1,0:T(8,128)S(1)} %get-tuple-element.8.gradient_ref, f32[8,128]{1,0:T(8,128)S(1)} %get-tuple-element.9.factor_ref, f32[32,128]{1,0:T(8,128)S(1)} %get-tuple-element.10.scales_ref, f32[128,4096]{1,0:T(8,128)S(1)} %get-tuple-element.11.outer_ref, ...), custom_call_target="tpu_custom_call" | custom-call | tf_op jit(solution)/shard_map/outer_step/pallas_call | solution.py:441

commit v4 on v3

--- a/solution.py
+++ b/solution.py
@@ -23,12 +23,11 @@
 grid_levels = 7.0
 
 CURVE = (
-    6.579736058540756,
-    -12.987862704441794,
-    12.207700561043827,
-    -6.688877467338575,
-    2.372163287039885,
-    -0.5163244078344457,
+    6.579723256002266,
+    -12.987145762286145,
+    12.194590761626122,
+    -6.583999071997054,
+    1.9907873039801487,
 )
 
 Y_STEPS = (2, 1, 3)
@@ -57,7 +56,7 @@
 
 def eighth_root(c):
     c = c.astype(F32)
-    size = jnp.exp(0.125 * jnp.log(jnp.maximum(jnp.abs(c), 1e-37)))
+    size = jnp.exp2(0.125 * jnp.log2(jnp.maximum(jnp.abs(c), 1e-37)))
     return jnp.where(c < 0.0, -size, size)
 
 
@@ -118,7 +117,7 @@
         for g in range(NY)
         for k, (src, dst) in enumerate(((local_hbm.at[0], local_v), (outer_hbm, outer_v)))
     ]
-    for c in [*loads, load_momentum]:
+    for c in loads:
         c.start()
 
     lasts = jnp.zeros((8, BLOCK), F32)
@@ -143,6 +142,7 @@
         )
     maxima[NY] = lasts
 
+    load_momentum.start()
     pl.semaphore_wait(barrier, len(friends))
 
     order = (4, 3, 5, 2, 6, 1, 7, 0)
@@ -167,7 +167,7 @@
         send(maxima.at[NY], maxima_y.at[i, 1], one_s.at[MY], one_r.at[MY], y=s)
     for i in range(NZ):
         send_raw_y(i)
-        if i < 2:
+        if i < 3:
             send_raw_z(i)
     landed(maxima_y, one_r.at[MY])
     for k, row in enumerate((y, NY)):
@@ -177,7 +177,7 @@
         max_own[k] = m
     for i, s in enumerate(Z_FAR):
         send(max_own, maxima_z.at[i], one_s.at[MZ], one_r.at[MZ], z=s)
-    for i in range(2, NZ - 1):
+    for i in range(3, NZ - 1):
         send_raw_z(i)
     landed(maxima_z, one_r.at[MZ])
     m, lasts = max_own[0], max_own[1]
@@ -218,7 +218,7 @@
                 total[:, lanes] = acc
             return 0
 
-        lax.fori_loop(0, near, encode, 0)
+        lax.fori_loop(0, near, encode, 0, unroll=True)
         if i < NZ - 1:
             send(partial.at[i], parts_z.at[i], one_s.at[PZ], one_r.at[PZ], z=order[i])
 
@@ -243,7 +243,7 @@
 
             return 0
 
-        lax.fori_loop(0, NY, encode, 0)
+        lax.fori_loop(0, NY, encode, 0, unroll=2)
         for k, s in enumerate(Y_STEPS):
             send(partial_y.at[lax.rem(y + s, NY)], parts_y.at[k], one_s.at[PY], one_r.at[PY], y=s)
 
@@ -252,6 +252,26 @@
     along_z()
     for i in range(5, NZ):
         along_y(i)
+    landed(maxima_y.at[:, 0], one_r.at[MA])
+    def spread_scale(g):
+        group_scale = (max_all[g] + epsilon) * (1.0 / (grid_levels * WORKERS))
+        for b in range(nb):
+            for r in range(nr // 8):
+                n = r * nb + b
+                spread[b, pl.ds(g * nr + r * 8, 8), :] = jnp.broadcast_to(
+                    group_scale[:, n : n + 1], (8, BLOCK)
+                )
+
+    for g in range(NY):
+        spread_scale(g)
+
+    stack = []
+    for g in range(NY):
+        for r in range(nr // 8):
+            turned = max_all[g] if r == 0 else pltpu.roll(max_all[g], BLOCK - r * nb, 1)
+            stack.append(turned)
+    scales_ref[...] = jnp.concatenate(stack, axis=0).T[:nb]
+
     landed(parts_z, one_r.at[PZ])
     landed(parts_y, one_r.at[PY])
 
@@ -301,18 +321,6 @@
     for s in Y_STEPS:
         send(ref, ref, one_s.at[GO], one_r.at[GO], y=s)
 
-    def spread_scale(g):
-        group_scale = (max_all[g] + epsilon) * (1.0 / (grid_levels * WORKERS))
-        for b in range(nb):
-            for r in range(nr // 8):
-                n = r * nb + b
-                spread[b, pl.ds(g * nr + r * 8, 8), :] = jnp.broadcast_to(
-                    group_scale[:, n : n + 1], (8, BLOCK)
-                )
-
-    landed(maxima_y.at[:, 0], one_r.at[MA])
-    spread_scale(0)
-    spread_scale(1)
     pass_on(0)
     pass_on(1)
     landed(raw_z.at[pl.ds(0, NY - 1)], one_r.at[GO])
@@ -322,22 +330,13 @@
     for i, s in enumerate(Y_STEPS):
         send(squares.at[1], squares_in.at[7 + i], one_s.at[QY], one_r.at[QY], y=s)
     pass_on(2)
-    spread_scale(2)
     pass_on(3)
-    spread_scale(3)
     pass_on(4)
+    pass_on(5)
+    pass_on(6)
     add_up(1, 7, 3, one_r.at[QY])
     for i, (a, b) in enumerate(CELL):
         send(squares.at[2], squares_in.at[10 + i], one_s.at[QC], one_r.at[QC], x=a, core=b)
-    pass_on(5)
-    pass_on(6)
-
-    stack = []
-    for g in range(NY):
-        for r in range(nr // 8):
-            turned = max_all[g] if r == 0 else pltpu.roll(max_all[g], BLOCK - r * nb, 1)
-            stack.append(turned)
-    scales_ref[...] = jnp.concatenate(stack, axis=0).T[:nb]
 
     for i in range(NZ):
         source = z if i == 0 else lax.rem(z + NZ - Z_NEAR[i - 1], NZ)
@@ -353,7 +352,7 @@
                 )
             return 0
 
-        lax.fori_loop(0, NY, decode, 0, unroll=2)
+        lax.fori_loop(0, NY, decode, 0, unroll=True)
 
     load_momentum.wait()
     add_up(2, 10, 7, one_r.at[QC])

time: 44.9 us -> 42.6 us (0.949)
  Pallas kernels: 44.1 us -> 41.9 us
    pallas_call x1, Pallas kernels: 41.9 us -> 39.6 us  [per_device(): pl.pallas_call(kernel, out_shape=(jax.ShapeDtypeStruct((rows, cols), F32)...]
where the time goes in v4:
time: 42.6 us; the launch traced here: 42.5 us
  Pallas kernels  41.9 us (98%)
  between operations  0.64 us (2%)
    pallas_call x1, Pallas kernels, per_device(): pl.pallas_call(kernel, out_shape=(jax.ShapeDtypeStruct((rows, cols), F32)...  39.6 us
    pallas_call x1, Pallas kernels, per_device(): pl.pallas_call(outer_step, out_shape=[jax.ShapeDtypeStruct((rows, cols),...  2.28 us

profile of v4, /device:TPU:1, one launch (start us, length us, event | category | flops | bytes accessed | tf_op | source)
XLA Modules:
  0.0 42.5 jit_solution(13552590902021487323)
XLA Ops:
  0.6 39.6 %synchronise.1 = (f32[128,4096]{1,0:T(8,128)S(1)}, f32[8,128]{1,0:T(8,128)S(1)}, f32[32,128]{1,0:T(8,128)S(1)}, f32[128,4096]{1,0:T(8,128)S(1)}, f32[128,4096]{1,0:T(8,128)S(1)}) custom-call(f32[128,4096]{1,0:T(8,128)} %outer_hbm.1, bf16[1,128,4096]{2,1,0:T(8,128)(2,1)} %local_hbm.1, f32[128,4096]{1,0:T(8,128)} %momentum_hbm.1), custom_call_target="tpu_custom_call" | custom-call | tf_op jit(solution)/shard_map/synchronise/pallas_call | solution.py:398
  40.2 2.3 %outer_step.1 = (f32[128,4096]{1,0:T(8,128)}, f32[128,4096]{1,0:T(8,128)}, f32[32,128]{1,0:T(8,128)}) custom-call(f32[128,4096]{1,0:T(8,128)S(1)} %get-tuple-element.8.gradient_ref, f32[8,128]{1,0:T(8,128)S(1)} %get-tuple-element.9.factor_ref, f32[32,128]{1,0:T(8,128)S(1)} %get-tuple-element.10.scales_ref, f32[128,4096]{1,0:T(8,128)S(1)} %get-tuple-element.11.outer_ref, ...), custom_call_target="tpu_custom_call" | custom-call | tf_op jit(solution)/shard_map/outer_step/pallas_call | solution.py:440

commit v5 on v4

--- a/solution.py
+++ b/solution.py
@@ -102,6 +102,15 @@
     def aligned(n, count=1):
         return pl.ds(pl.multiple_of(n * BLOCK, BLOCK), count * BLOCK)
 
+    load_momentum = pltpu.make_async_copy(momentum_hbm, momentum_v, load_sem.at[2, 0])
+    loads = [
+        pltpu.make_async_copy(src.at[pl.ds(g * nr, nr)], dst.at[pl.ds(g * nr, nr)], load_sem.at[k, g])
+        for g in range(NY)
+        for k, (src, dst) in enumerate(((local_hbm.at[0], local_v), (outer_hbm, outer_v)))
+    ]
+    for c in loads:
+        c.start()
+
     barrier = pltpu.get_barrier_semaphore()
     friends = (
         [dict(y=s) for s in range(1, NY)]
@@ -110,15 +119,6 @@
     )
     for f in friends:
         pl.semaphore_signal(barrier, inc=1, device_id=peer(**f), device_id_type=MESH)
-
-    load_momentum = pltpu.make_async_copy(momentum_hbm, momentum_v, load_sem.at[2, 0])
-    loads = [
-        pltpu.make_async_copy(src.at[pl.ds(g * nr, nr)], dst.at[pl.ds(g * nr, nr)], load_sem.at[k, g])
-        for g in range(NY)
-        for k, (src, dst) in enumerate(((local_hbm.at[0], local_v), (outer_hbm, outer_v)))
-    ]
-    for c in loads:
-        c.start()
 
     lasts = jnp.zeros((8, BLOCK), F32)
     for g in range(NY):

time: 42.6 us -> 42.3 us (level)
  no operation moved by 1% of the time
where the time goes in v5:
time: 42.3 us; the launch traced here: 42.2 us
  Pallas kernels  41.6 us (98%)
  between operations  0.64 us (2%)
    pallas_call x1, Pallas kernels, per_device(): pl.pallas_call(kernel, out_shape=(jax.ShapeDtypeStruct((rows, cols), F32)...  39.3 us
    pallas_call x1, Pallas kernels, per_device(): pl.pallas_call(outer_step, out_shape=[jax.ShapeDtypeStruct((rows, cols),...  2.28 us

profile of v5, /device:TPU:1, one launch (start us, length us, event | category | flops | bytes accessed | tf_op | source)
XLA Modules:
  0.0 42.2 jit_solution(9506468301578629212)
XLA Ops:
  0.6 39.3 %synchronise.1 = (f32[128,4096]{1,0:T(8,128)S(1)}, f32[8,128]{1,0:T(8,128)S(1)}, f32[32,128]{1,0:T(8,128)S(1)}, f32[128,4096]{1,0:T(8,128)S(1)}, f32[128,4096]{1,0:T(8,128)S(1)}) custom-call(f32[128,4096]{1,0:T(8,128)} %outer_hbm.1, bf16[1,128,4096]{2,1,0:T(8,128)(2,1)} %local_hbm.1, f32[128,4096]{1,0:T(8,128)} %momentum_hbm.1), custom_call_target="tpu_custom_call" | custom-call | tf_op jit(solution)/shard_map/synchronise/pallas_call | solution.py:398
  40.0 2.3 %outer_step.1 = (f32[128,4096]{1,0:T(8,128)}, f32[128,4096]{1,0:T(8,128)}, f32[32,128]{1,0:T(8,128)}) custom-call(f32[128,4096]{1,0:T(8,128)S(1)} %get-tuple-element.8.gradient_ref, f32[8,128]{1,0:T(8,128)S(1)} %get-tuple-element.9.factor_ref, f32[32,128]{1,0:T(8,128)S(1)} %get-tuple-element.10.scales_ref, f32[128,4096]{1,0:T(8,128)S(1)} %get-tuple-element.11.outer_ref, ...), custom_call_target="tpu_custom_call" | custom-call | tf_op jit(solution)/shard_map/outer_step/pallas_call | solution.py:440

commit v6 on v5

--- a/solution.py
+++ b/solution.py
@@ -115,6 +115,7 @@
     friends = (
         [dict(y=s) for s in range(1, NY)]
         + [dict(z=s) for s in range(1, NZ)]
+        + [dict(y=a, z=b) for a in range(1, NY) for b in (1, NZ - 1)]
         + [dict(x=a, core=b) for a, b in CELL]
     )
     for f in friends:
@@ -298,8 +299,9 @@
         source = lax.rem(z + NZ - Z_NEAR[i], NZ)
         ref = gathered.at[y, source, most]
         landed(ref, gz_r.at[i])
-        for s in Y_STEPS:
-            send(ref, ref, one_s.at[GY], gy_r.at[i], y=s)
+        if i >= 2:
+            for s in Y_STEPS:
+                send(ref, ref, one_s.at[GY], gy_r.at[i], y=s)
 
     def pass_last(i):
         ref = gathered.at[:, z, near]
@@ -315,14 +317,18 @@
     for i, s in enumerate(Z_NEAR):
         send(squares.at[0], squares_in.at[i], one_s.at[QZ], one_r.at[QZ], z=s)
     ref = gathered.at[y, z, most]
-    for i, s in enumerate(Z_NEAR):
-        send(ref, ref, one_s.at[GZ], gz_r.at[i], z=s)
+    for i in reversed(range(2, NZ - 1)):
+        send(ref, ref, one_s.at[GZ], gz_r.at[i], z=Z_NEAR[i])
     ref = gathered.at[y, z]
     for s in Y_STEPS:
         send(ref, ref, one_s.at[GO], one_r.at[GO], y=s)
-
-    pass_on(0)
-    pass_on(1)
+    ref = gathered.at[y, z, most]
+    for i in range(2):
+        for s in Y_STEPS:
+            send(ref, ref, one_s.at[GY], gy_r.at[i], y=s, z=Z_NEAR[i])
+    for i in range(2):
+        send(ref, ref, one_s.at[GZ], gz_r.at[i], z=Z_NEAR[i])
+
     landed(raw_z.at[pl.ds(0, NY - 1)], one_r.at[GO])
     for i in range(NZ - 1):
         pass_last(i)
@@ -337,6 +343,9 @@
     add_up(1, 7, 3, one_r.at[QY])
     for i, (a, b) in enumerate(CELL):
         send(squares.at[2], squares_in.at[10 + i], one_s.at[QC], one_r.at[QC], x=a, core=b)
+
+    pass_on(0)
+    pass_on(1)
 
     for i in range(NZ):
         source = z if i == 0 else lax.rem(z + NZ - Z_NEAR[i - 1], NZ)

time: 42.3 us -> 41.2 us (0.974)
  Pallas kernels: 41.6 us -> 40.4 us
    pallas_call x1, Pallas kernels: 39.3 us -> 38.1 us  [per_device(): pl.pallas_call(kernel, out_shape=(jax.ShapeDtypeStruct((rows, cols), F32)...]
where the time goes in v6:
time: 41.2 us; the launch traced here: 41.1 us
  Pallas kernels  40.4 us (98%)
  between operations  0.64 us (2%)
    pallas_call x1, Pallas kernels, per_device(): pl.pallas_call(kernel, out_shape=(jax.ShapeDtypeStruct((rows, cols), F32)...  38.1 us
    pallas_call x1, Pallas kernels, per_device(): pl.pallas_call(outer_step, out_shape=[jax.ShapeDtypeStruct((rows, cols),...  2.28 us

profile of v6, /device:TPU:1, one launch (start us, length us, event | category | flops | bytes accessed | tf_op | source)
XLA Modules:
  0.0 41.1 jit_solution(11926106922585941780)
XLA Ops:
  0.6 38.1 %synchronise.1 = (f32[128,4096]{1,0:T(8,128)S(1)}, f32[8,128]{1,0:T(8,128)S(1)}, f32[32,128]{1,0:T(8,128)S(1)}, f32[128,4096]{1,0:T(8,128)S(1)}, f32[128,4096]{1,0:T(8,128)S(1)}) custom-call(f32[128,4096]{1,0:T(8,128)} %outer_hbm.1, bf16[1,128,4096]{2,1,0:T(8,128)(2,1)} %local_hbm.1, f32[128,4096]{1,0:T(8,128)} %momentum_hbm.1), custom_call_target="tpu_custom_call" | custom-call | tf_op jit(solution)/shard_map/synchronise/pallas_call | solution.py:407
  38.8 2.3 %outer_step.1 = (f32[128,4096]{1,0:T(8,128)}, f32[128,4096]{1,0:T(8,128)}, f32[32,128]{1,0:T(8,128)}) custom-call(f32[128,4096]{1,0:T(8,128)S(1)} %get-tuple-element.8.gradient_ref, f32[8,128]{1,0:T(8,128)S(1)} %get-tuple-element.9.factor_ref, f32[32,128]{1,0:T(8,128)S(1)} %get-tuple-element.10.scales_ref, f32[128,4096]{1,0:T(8,128)S(1)} %get-tuple-element.11.outer_ref, ...), custom_call_target="tpu_custom_call" | custom-call | tf_op jit(solution)/shard_map/outer_step/pallas_call | solution.py:449

commit v7 on v6

--- a/solution.py
+++ b/solution.py
@@ -330,13 +330,13 @@
         send(ref, ref, one_s.at[GZ], gz_r.at[i], z=Z_NEAR[i])
 
     landed(raw_z.at[pl.ds(0, NY - 1)], one_r.at[GO])
-    for i in range(NZ - 1):
-        pass_last(i)
     add_up(0, 0, 7, one_r.at[QZ])
     for i, s in enumerate(Y_STEPS):
         send(squares.at[1], squares_in.at[7 + i], one_s.at[QY], one_r.at[QY], y=s)
     pass_on(2)
     pass_on(3)
+    for i in range(NZ - 1):
+        pass_last(i)
     pass_on(4)
     pass_on(5)
     pass_on(6)
@@ -394,7 +394,7 @@
         params_v[i] = outer_ref[where] - outer_rate * (clipped + outer_decay * after)
         for k, (src, dst) in enumerate(((params_v, params_hbm), (momentum_v, momentum_hbm))):
             copies.append(pltpu.make_async_copy(src.at[i], dst.at[where], sem.at[2 * i + k]))
-            copies[-1].start()
+            copies[-1].start(priority=k)
     for c in copies:
         c.wait()
 

time: 41.2 us -> 41.2 us (level)
  no operation moved by 1% of the time
where the time goes in v7:
time: 41.2 us
  Pallas kernels  40.5 us (98%)
  between operations  0.64 us (2%)
    pallas_call x1, Pallas kernels, per_device(): pl.pallas_call(kernel, out_shape=(jax.ShapeDtypeStruct((rows, cols), F32)...  38.2 us
    pallas_call x1, Pallas kernels, per_device(): pl.pallas_call(outer_step, out_shape=[jax.ShapeDtypeStruct((rows, cols),...  2.28 us

profile of v7, /device:TPU:1, one launch (start us, length us, event | category | flops | bytes accessed | tf_op | source)
XLA Modules:
  0.0 41.2 jit_solution(3869316219019765849)
XLA Ops:
  0.6 38.2 %synchronise.1 = (f32[128,4096]{1,0:T(8,128)S(1)}, f32[8,128]{1,0:T(8,128)S(1)}, f32[32,128]{1,0:T(8,128)S(1)}, f32[128,4096]{1,0:T(8,128)S(1)}, f32[128,4096]{1,0:T(8,128)S(1)}) custom-call(f32[128,4096]{1,0:T(8,128)} %outer_hbm.1, bf16[1,128,4096]{2,1,0:T(8,128)(2,1)} %local_hbm.1, f32[128,4096]{1,0:T(8,128)} %momentum_hbm.1), custom_call_target="tpu_custom_call" | custom-call | tf_op jit(solution)/shard_map/synchronise/pallas_call | solution.py:407
  38.9 2.3 %outer_step.1 = (f32[128,4096]{1,0:T(8,128)}, f32[128,4096]{1,0:T(8,128)}, f32[32,128]{1,0:T(8,128)}) custom-call(f32[128,4096]{1,0:T(8,128)S(1)} %get-tuple-element.8.gradient_ref, f32[8,128]{1,0:T(8,128)S(1)} %get-tuple-element.9.factor_ref, f32[32,128]{1,0:T(8,128)S(1)} %get-tuple-element.10.scales_ref, f32[128,4096]{1,0:T(8,128)S(1)} %get-tuple-element.11.outer_ref, ...), custom_call_target="tpu_custom_call" | custom-call | tf_op jit(solution)/shard_map/outer_step/pallas_call | solution.py:449
